TPU v7x, 32 devices: a whole 2x2x4 slice. The times are simulated.
32 devices in a mesh: seq: 2 (over x), head: 4 (over z), dp: 4 (over y, core).
Axes of the slice: x: 2, y: 2, z: 4, core: 2. Of those that a mesh axis runs over, the one named last changes fastest.
Arguments:
- queries: bfloat16 [4, 512, 64, 128], P('dp', 'seq', 'head'), may hold values from -6 to 6
- keys: bfloat16 [4, 512, 8, 128], P('dp', 'seq', 'head'), may hold values from -6 to 6
- values: bfloat16 [4, 512, 8, 128], P('dp', 'seq', 'head'), may hold values from -6 to 6
- attn_out: bfloat16 [4, 512, 64, 128], P('dp', 'seq', 'head'), may hold values from -6 to 6
- out_grad: bfloat16 [4, 512, 64, 128], P('dp', 'seq', 'head'), may hold values from -6 to 6
- gate_values: float32 [4, 64, 512], P('dp', 'head', 'seq'), may hold values from 0.05 to 0.95
- log_totals: float32 [4, 64, 512], P('dp', 'head', 'seq'), may hold values from 3 to 5
- hidden: bfloat16 [4, 512, 5120], P('dp', 'seq', 'head'), may hold values from -6 to 6
- block_ids: int32 [4, 8, 8, 16], P('dp', 'seq', 'head'), may hold values from 0 to 7, as said below
- block_valid: int32 [4, 8, 8, 16], P('dp', 'seq', 'head'), may hold values from 0 to 1
Outputs:
- query_grad: bfloat16 [4, 512, 64, 128], P('dp', 'seq', 'head')
- key_grad: bfloat16 [4, 512, 8, 128], P('dp', 'seq', 'head')
- value_grad: bfloat16 [4, 512, 8, 128], P('dp', 'seq', 'head')
- gate_weight_grad: float32 [64, 5120], P(None, 'head')
Inputs may be any that keep to these rules, and one draw needn't show every extreme that they name: `block_ids`: for query tile t and key head k, the slots whose block_valid is 1 name distinct blocks of index at most t, among them block t itself and block 0; exactly min(16, t + 1) slots are valid. The ids of the other slots are any blocks, and may repeat a valid one.
All inputs are finite; a program needn't handle non-finite values.
Results may differ from a plain program's by a relative error of at most 0.025.
Values may be sent and summed in bfloat16 or wider, within the bound.
A program may use at most 128 MiB of HBM per device.

v0:
```python
import math
import jax
import jax.numpy as jnp
from jax import lax
from jax.sharding import PartitionSpec as P


def on_device(
    queries,
    keys,
    values,
    attn_out,
    out_grad,
    gate_values,
    log_totals,
    hidden,
    block_ids,
    block_valid,
):
    tokens_here = queries.shape[1]
    heads_here = queries.shape[2]
    kv_heads = keys.shape[2]
    head_width = queries.shape[3]
    group_size = heads_here // kv_heads
    tiles_here = block_ids.shape[1]
    block_rows = tokens_here // tiles_here
    seq_count = lax.axis_size("seq")
    all_blocks = tiles_here * seq_count
    factor = head_width ** (-0.5)
    chosen = block_ids[0]
    usable = block_valid[0] > 0
    head_rows = jnp.arange(kv_heads, dtype=jnp.int32)[None, :, None]
    offsets = jnp.arange(block_rows, dtype=jnp.int32)
    whole_keys, whole_values = (
        lax.all_gather(keys, "seq", axis=1, tiled=True),
        lax.all_gather(values, "seq", axis=1, tiled=True),
    )
    key_sel = whole_keys[0].reshape(all_blocks, block_rows, kv_heads, head_width)[
        chosen, :, head_rows, :
    ]
    value_sel = whole_values[0].reshape(all_blocks, block_rows, kv_heads, head_width)[
        chosen, :, head_rows, :
    ]
    query_tiles = queries[0].reshape(tiles_here, block_rows, kv_heads, group_size, head_width)
    output_tiles = attn_out[0].reshape(tiles_here, block_rows, kv_heads, group_size, head_width)
    upstream_tiles = out_grad[0].reshape(tiles_here, block_rows, kv_heads, group_size, head_width)
    gate_tiles = jnp.transpose(
        gate_values[0].reshape(kv_heads, group_size, tiles_here, block_rows), (2, 0, 1, 3)
    )
    total_tiles = jnp.transpose(
        log_totals[0].reshape(kv_heads, group_size, tiles_here, block_rows), (2, 0, 1, 3)
    )
    tile_numbers = lax.axis_index("seq") * tiles_here + jnp.arange(tiles_here, dtype=jnp.int32)

    def tile_math(tile_items):
        (
            tile_number,
            query_tile,
            output_tile,
            upstream,
            gate_tile,
            totals,
            picked,
            usable_tile,
            key_tile,
            value_tile,
        ) = tile_items
        gates_by_row = jnp.transpose(gate_tile, (2, 0, 1))
        grad_output = (gates_by_row[..., None] * upstream.astype(jnp.float32)).astype(jnp.bfloat16)
        output_wide = output_tile.astype(jnp.float32)
        row_delta = jnp.transpose(
            jnp.sum(grad_output.astype(jnp.float32) * output_wide, axis=-1), (1, 2, 0)
        )
        gate_grad = jnp.sum(upstream.astype(jnp.float32) * output_wide, axis=-1)
        logit_grad = (gate_grad * gates_by_row * (1.0 - gates_by_row)).astype(jnp.bfloat16)
        scores = (
            jnp.einsum("ikgd,knjd->kginj", query_tile, key_tile, preferred_element_type=jnp.float32)
            * factor
        )
        query_pos = tile_number * block_rows + offsets
        key_pos = picked[..., None] * block_rows + offsets
        allowed = usable_tile[:, None, :, None] & (
            key_pos[:, None, :, :] <= query_pos[None, :, None, None]
        )
        probability = jnp.where(allowed[:, None], jnp.exp(scores - totals[..., None, None]), 0.0)
        prob_grad = jnp.einsum(
            "ikgd,knjd->kginj", grad_output, value_tile, preferred_element_type=jnp.float32
        )
        dscore = (probability * (prob_grad - row_delta[..., None, None])).astype(jnp.bfloat16)
        prob_low = probability.astype(jnp.bfloat16)
        query_part = (
            jnp.einsum("kginj,knjd->ikgd", dscore, key_tile, preferred_element_type=jnp.float32)
            * factor
        ).astype(jnp.bfloat16)
        key_part = (
            jnp.einsum("kginj,ikgd->knjd", dscore, query_tile, preferred_element_type=jnp.float32)
            * factor
        )
        value_part = jnp.einsum(
            "kginj,ikgd->knjd", prob_low, grad_output, preferred_element_type=jnp.float32
        )
        return (query_part, logit_grad, jnp.concatenate([key_part, value_part], axis=-1))

    def tile_step(partial_value, tile_items):
        query_part, logit_grad, paired = tile_math(tile_items)
        return (partial_value, (query_part, logit_grad, paired))

    tile_items = (
        tile_numbers,
        query_tiles,
        output_tiles,
        upstream_tiles,
        gate_tiles,
        total_tiles,
        chosen,
        usable,
        key_sel,
        value_sel,
    )
    unused, (query_parts, logit_parts, paired_all) = lax.scan(
        tile_step, jnp.zeros((), jnp.float32), tile_items
    )
    span_blocks = tokens_here * lax.axis_size("seq") // block_rows
    target = chosen
    target = jnp.where((target >= 0) & (target < span_blocks), target, span_blocks)
    holder = jnp.zeros((span_blocks, block_rows, kv_heads, 2 * head_width), jnp.float32)
    holder = holder.at[target, :, head_rows, :].add(paired_all, mode="drop")
    summed = lax.psum_scatter(
        holder.reshape(tokens_here * lax.axis_size("seq"), kv_heads, 2 * head_width).astype(
            jnp.bfloat16
        ),
        "seq",
        scatter_dimension=0,
        tiled=True,
    ).astype(jnp.float32)
    query_grad = query_parts.reshape(1, tokens_here, heads_here, head_width)
    logit_rows = jnp.transpose(logit_parts.reshape(tokens_here, heads_here))[None]
    every_logit = lax.all_gather(logit_rows, "head", axis=1, tiled=True)
    weight_part = jnp.dot(every_logit[0], hidden[0], preferred_element_type=jnp.float32)
    weight_scale = 1.0 / math.sqrt(lax.axis_size("dp") * seq_count * tokens_here)
    gate_weight_grad = lax.psum(weight_part, ("seq", "dp")) * weight_scale
    key_grad = summed[None, :, :, :head_width].astype(jnp.bfloat16)
    value_grad = summed[None, :, :, head_width:].astype(jnp.bfloat16)
    return (query_grad, key_grad, value_grad, gate_weight_grad)


def solution(mesh):
    return jax.shard_map(
        on_device,
        mesh=mesh,
        in_specs=(
            P("dp", "seq", "head", None),
            P("dp", "seq", "head", None),
            P("dp", "seq", "head", None),
            P("dp", "seq", "head", None),
            P("dp", "seq", "head", None),
            P("dp", "head", "seq"),
            P("dp", "head", "seq"),
            P("dp", "seq", "head"),
            P("dp", "seq", "head", None),
            P("dp", "seq", "head", None),
        ),
        out_specs=(
            P("dp", "seq", "head", None),
            P("dp", "seq", "head", None),
            P("dp", "seq", "head", None),
            P(None, "head"),
        ),
        check_vma=False,
    )
```

profile of v0, /device:TPU:0, one launch (start us, length us, event | category | flops | bytes accessed | tf_op | source)
XLA Modules:
  0.0 180.2 jit_solution(4722716227157090044)
XLA Ops:
  9.0 7.1 %all_gather.9 = bf16[1,512,2,128]{3,1,2,0:T(8,128)(2,1)S(1)} all-gather(bf16[1,256,2,128]{3,1,2,0:T(8,128)(2,1)S(1)} %copy.32), channel_id=1, replica_groups=mesh['seq'=2,'head'=4,'dp'=4] {'seq'}, dimensions={1}, use_global_device_ids=true | all-gather | bytes 393216 | tf_op jit(solution)/shard_map/all_gather | solution.py:35
  19.4 5.6 %all_gather.10 = bf16[1,512,2,128]{3,1,2,0:T(8,128)(2,1)S(1)} all-gather(bf16[1,256,2,128]{3,1,2,0:T(8,128)(2,1)S(1)} %copy.35), channel_id=1, replica_groups=mesh['seq'=2,'head'=4,'dp'=4] {'seq'}, dimensions={1}, use_global_device_ids=true | all-gather | bytes 393216 | tf_op jit(solution)/shard_map/all_gather | solution.py:36
  26.1 2.3 %gather_fusion.1 = bf16[128,64,128]{2,1,0:T(8,128)(2,1)} fusion(bf16[8,64,2,128]{3,1,2,0:T(8,128)(2,1)S(1)} %copy.36, s32[128]{0:T(128)S(1)} %reshape.124), kind=kCustom, calls=%fused_computation.1 | custom fusion | bytes 4195328 | tf_op jit(solution)/shard_map/gather | solution.py:41
  28.6 69.9 %while.16 = (s32[]{:T(128)}, bf16[4,64,2,8,128]{4,3,2,1,0:T(8,128)(2,1)}, bf16[4,64,2,8]{1,3,2,0:T(8,128)(2,1)S(1)}, f32[4,2,16,64,256]{4,3,2,1,0:T(8,128)}, bf1...) while((s32[]{:T(128)}, ...), condition=%wide.region_3.4_spmd.clone.clone, body=%wide.region_0.3_spmd.clone.clone.sunk | while | flops 1355944064 | bytes 33248452 | solution.py:120
  35.0 4.0 %fusion.82 = bf16[2,8,64,16,64]{2,4,1,3,0:T(8,128)(2,1)S(1)} fusion(f32[2,16,64,64,8]{3,2,4,1,0:T(8,128)S(1)} %fusion.78, f32[2,8,64]{2,1,0:T(8,128)S(1)} %bitcast.222, f32[2,8,64]{2,1,0:T(8,128)S(1)} %bitcast.223, pred[2,64,16,64]{1,3,2,0:T(8,128)(4,1)S(1)} %compare_and_fusion.2, bf16[4,2,16,64,128]{4,3,2,1,0:T(8,128)(2,1)} %get-tuple-element.380, ...), kind=kOutput, calls=%fused_computation.6.clone.1 | convolution fusion | flops 275120128 | bytes 7221252 | tf_op jit(solution)/shard_map/while/body/eval_jaxpr/ikgd,knjd->kginj/dot_general | solution.py:86
  39.0 1.3 fusion.83
  41.2 2.4 %fusion.85 = f32[2,16,64,128]{3,2,1,0:T(8,128)S(1)} fusion(f32[2,16,64,64,8]{3,2,4,1,0:T(8,128)S(1)} %fusion.78, f32[2,8,64]{2,1,0:T(8,128)S(1)} %bitcast.224, pred[2,64,16,64]{1,3,2,0:T(8,128)(4,1)S(1)} %compare_and_fusion.2, f32[64,2,8]{0,2,1:T(8,128)S(1)} %bitcast.216, bf16[1,64,2,8,128]{4,3,2,1,0:T(8,128)(2,1)S(1)} %get-tuple-element.332), kind=kOutput, calls=%fused_computation.17.clone.1 | convolution fusion | flops 273022976 | bytes 5644288 | tf_op jit(solution)/shard_map/while/body/eval_jaxpr/kginj,ikgd->knjd/dot_general | solution.py:99
  44.6 1.5 fusion.87
  52.4 4.0 %fusion.82 = bf16[2,8,64,16,64]{2,4,1,3,0:T(8,128)(2,1)S(1)} fusion(f32[2,16,64,64,8]{3,2,4,1,0:T(8,128)S(1)} %fusion.78, f32[2,8,64]{2,1,0:T(8,128)S(1)} %bitcast.222, f32[2,8,64]{2,1,0:T(8,128)S(1)} %bitcast.223, pred[2,64,16,64]{1,3,2,0:T(8,128)(4,1)S(1)} %compare_and_fusion.2, bf16[4,2,16,64,128]{4,3,2,1,0:T(8,128)(2,1)} %get-tuple-element.380, ...), kind=kOutput, calls=%fused_computation.6.clone.1 | convolution fusion | flops 275120128 | bytes 7221252 | tf_op jit(solution)/shard_map/while/body/eval_jaxpr/ikgd,knjd->kginj/dot_general | solution.py:86
  56.5 1.3 fusion.83
  58.7 2.4 %fusion.85 = f32[2,16,64,128]{3,2,1,0:T(8,128)S(1)} fusion(f32[2,16,64,64,8]{3,2,4,1,0:T(8,128)S(1)} %fusion.78, f32[2,8,64]{2,1,0:T(8,128)S(1)} %bitcast.224, pred[2,64,16,64]{1,3,2,0:T(8,128)(4,1)S(1)} %compare_and_fusion.2, f32[64,2,8]{0,2,1:T(8,128)S(1)} %bitcast.216, bf16[1,64,2,8,128]{4,3,2,1,0:T(8,128)(2,1)S(1)} %get-tuple-element.332), kind=kOutput, calls=%fused_computation.17.clone.1 | convolution fusion | flops 273022976 | bytes 5644288 | tf_op jit(solution)/shard_map/while/body/eval_jaxpr/kginj,ikgd->knjd/dot_general | solution.py:99
  62.1 1.4 fusion.87
  69.9 4.0 %fusion.82 = bf16[2,8,64,16,64]{2,4,1,3,0:T(8,128)(2,1)S(1)} fusion(f32[2,16,64,64,8]{3,2,4,1,0:T(8,128)S(1)} %fusion.78, f32[2,8,64]{2,1,0:T(8,128)S(1)} %bitcast.222, f32[2,8,64]{2,1,0:T(8,128)S(1)} %bitcast.223, pred[2,64,16,64]{1,3,2,0:T(8,128)(4,1)S(1)} %compare_and_fusion.2, bf16[4,2,16,64,128]{4,3,2,1,0:T(8,128)(2,1)} %get-tuple-element.380, ...), kind=kOutput, calls=%fused_computation.6.clone.1 | convolution fusion | flops 275120128 | bytes 7221252 | tf_op jit(solution)/shard_map/while/body/eval_jaxpr/ikgd,knjd->kginj/dot_general | solution.py:86
  73.9 1.3 fusion.83
  76.1 2.4 %fusion.85 = f32[2,16,64,128]{3,2,1,0:T(8,128)S(1)} fusion(f32[2,16,64,64,8]{3,2,4,1,0:T(8,128)S(1)} %fusion.78, f32[2,8,64]{2,1,0:T(8,128)S(1)} %bitcast.224, pred[2,64,16,64]{1,3,2,0:T(8,128)(4,1)S(1)} %compare_and_fusion.2, f32[64,2,8]{0,2,1:T(8,128)S(1)} %bitcast.216, bf16[1,64,2,8,128]{4,3,2,1,0:T(8,128)(2,1)S(1)} %get-tuple-element.332), kind=kOutput, calls=%fused_computation.17.clone.1 | convolution fusion | flops 273022976 | bytes 5644288 | tf_op jit(solution)/shard_map/while/body/eval_jaxpr/kginj,ikgd->knjd/dot_general | solution.py:99
  79.5 1.5 fusion.87
  87.3 4.0 %fusion.82 = bf16[2,8,64,16,64]{2,4,1,3,0:T(8,128)(2,1)S(1)} fusion(f32[2,16,64,64,8]{3,2,4,1,0:T(8,128)S(1)} %fusion.78, f32[2,8,64]{2,1,0:T(8,128)S(1)} %bitcast.222, f32[2,8,64]{2,1,0:T(8,128)S(1)} %bitcast.223, pred[2,64,16,64]{1,3,2,0:T(8,128)(4,1)S(1)} %compare_and_fusion.2, bf16[4,2,16,64,128]{4,3,2,1,0:T(8,128)(2,1)} %get-tuple-element.380, ...), kind=kOutput, calls=%fused_computation.6.clone.1 | convolution fusion | flops 275120128 | bytes 7221252 | tf_op jit(solution)/shard_map/while/body/eval_jaxpr/ikgd,knjd->kginj/dot_general | solution.py:86
  91.4 1.3 fusion.83
  93.6 2.4 %fusion.85 = f32[2,16,64,128]{3,2,1,0:T(8,128)S(1)} fusion(f32[2,16,64,64,8]{3,2,4,1,0:T(8,128)S(1)} %fusion.78, f32[2,8,64]{2,1,0:T(8,128)S(1)} %bitcast.224, pred[2,64,16,64]{1,3,2,0:T(8,128)(4,1)S(1)} %compare_and_fusion.2, f32[64,2,8]{0,2,1:T(8,128)S(1)} %bitcast.216, bf16[1,64,2,8,128]{4,3,2,1,0:T(8,128)(2,1)S(1)} %get-tuple-element.332), kind=kOutput, calls=%fused_computation.17.clone.1 | convolution fusion | flops 273022976 | bytes 5644288 | tf_op jit(solution)/shard_map/while/body/eval_jaxpr/kginj,ikgd->knjd/dot_general | solution.py:99
  96.9 1.5 fusion.87
  98.5 13.6 %all-gather = bf16[64,256]{1,0:T(8,128)(2,1)S(1)} all-gather(bf16[16,256]{1,0:T(8,128)(2,1)S(1)} %bitcast.227), channel_id=2, replica_groups=mesh['seq'=2,'head'=4,'dp'=4] {'head'}, dimensions={0}, use_global_device_ids=true | all-gather | bytes 40960 | tf_op jit(solution)/shard_map/all_gather | solution.py:138
  113.4 19.1 %scatter_fusion = f32[8,64,2,256]{3,1,2,0:T(8,128)S(1)} fusion(f32[8,64,2,256]{3,1,2,0:T(8,128)S(1)} %broadcast_in_dim.53, s32[128]{0:T(128)S(1)} %reshape.136, f32[128,64,256]{2,1,0:T(8,128)} %bitcast.210), kind=kCustom, calls=%fused_computation.2 | custom fusion | flops 2097152 | bytes 25166848 | tf_op jit(solution)/shard_map/scatter-add | solution.py:127
  133.4 35.1 %all-reduce.2.cloned.1.call-done = f32[64,1280]{1,0:T(8,128)} async-done(((f32[64,1280]{1,0:T(8,128)}), f32[64,1280]{1,0:T(8,128)}) %all-reduce.2.cloned.1.call-update) | async-done | bytes 327696 | tf_op jit(solution)/shard_map/psum | solution.py:141
  168.5 1.7 broadcast_multiply_fusion
  (89 shorter events, 40.3 us)
Async XLA Ops:
  8.0 104.2 %copy-start = (bf16[1,256,1280]{2,1,0:T(8,128)(2,1)S(1)}, bf16[1,256,1280]{2,1,0:T(8,128)(2,1)}, u32[]{:S(2)}) copy-start(bf16[1,256,1280]{2,1,0:T(8,128)(2,1)} %param.19) | copy-start | bytes 1966084
  8.0 20.5 %copy-start.1 = (f32[1,16,256]{2,1,0:T(8,128)S(1)}, f32[1,16,256]{2,1,0:T(8,128)}, u32[]{:S(2)}) copy-start(f32[1,16,256]{2,1,0:T(8,128)} %param.17) | copy-start | bytes 49156
  8.0 160.4 %all-reduce.2.cloned.1.call-start = ((), (), s32[]{:S(2)}) async-start(), calls=%async_computation.2 | async-start | bytes 655360 | tf_op jit(solution)/shard_map/psum | solution.py:141
  113.2 57.0 %reduce-scatter.2.cloned.1.call-start = ((), (), s32[]{:S(2)}) async-start(), calls=%async_computation.1 | async-start | bytes 786432 | tf_op jit(solution)/shard_map/reduce_scatter | solution.py:128
Sparse Core Ops, SparseCore 0:
  113.3 55.1 all-reduce.1
Sparse Core Ops, SparseCore 1:
  133.5 15.6 reduce-scatter.1
where the time goes:
time: 181 us; the launch traced here: 180 us
  matrix products  40.9 us (23%)
  other arithmetic  35.2 us (19%)
  waiting for transfers between devices  35.1 us (19%)
  blocking collectives  26.4 us (15%)
  local copies, waits for them, and re-layouts  24.1 us (13%)
  between operations  15.6 us (9%)
  loops' own time  2.88 us (2%)
    psum x1, waiting for transfers between devices, on_device(): gate_weight_grad = lax.psum(weight_part, ('seq', 'dp')) * weight_scale  35.1 us
    scatter-add x1, other arithmetic, on_device(): holder = holder.at[target, :, head_rows, :].add(paired_all, mode='drop')  19.1 us
    dot_general x4, matrix products, tile_math(): jnp.einsum('ikgd,knjd->kginj', grad_output, value_tile, preferred_element...  16.1 us
    all_gather x1, blocking collectives, on_device(): every_logit = lax.all_gather(logit_rows, 'head', axis=1, tiled=True)  13.6 us
    dynamic_slice x16, local copies, waits for them, and re-layouts, on_device(): lax.scan(tile_step, jnp.zeros((), jnp.float32), tile_items)  10.6 us
    dot_general x4, matrix products, tile_math(): jnp.einsum('kginj,ikgd->knjd', prob_low, grad_output, preferred_element_t...  9.55 us
    all_gather x1, blocking collectives, on_device(): lax.all_gather(keys, 'seq', axis=1, tiled=True)  7.12 us
    dynamic_update_slice x8, other arithmetic, on_device(): lax.scan(tile_step, jnp.zeros((), jnp.float32), tile_items)  5.93 us
  transfers between devices with their start and end apart: 2, of which 1 were waited for; matrix products, arithmetic and copies ran while one was open for 12% of the time, Pallas kernels for 0%

commit v1 on v0

--- a/solution.py
+++ b/solution.py
@@ -138,7 +138,9 @@
     every_logit = lax.all_gather(logit_rows, "head", axis=1, tiled=True)
     weight_part = jnp.dot(every_logit[0], hidden[0], preferred_element_type=jnp.float32)
     weight_scale = 1.0 / math.sqrt(lax.axis_size("dp") * seq_count * tokens_here)
-    gate_weight_grad = lax.psum(weight_part, ("seq", "dp")) * weight_scale
+    gate_weight_grad = (
+        lax.psum(lax.psum(weight_part, axis_name="dp"), axis_name="seq") * weight_scale
+    )
     key_grad = summed[None, :, :, :head_width].astype(jnp.bfloat16)
     value_grad = summed[None, :, :, head_width:].astype(jnp.bfloat16)
     return (query_grad, key_grad, value_grad, gate_weight_grad)

time: 181 us -> 200 us (1.10)
  waiting for transfers between devices: 35.1 us -> 55.3 us
    reduce_scatter x1, waiting for transfers between devices: 0.01 us -> 15.2 us  [on_device(): lax.psum_scatter(holder.reshape(tokens_here * lax.axis_size('seq'), kv_he...]
    psum x1 -> x2, waiting for transfers between devices: 35.1 us -> 40.1 us  [the longest x1 33.7 us: on_device(): lax.psum(weight_part, axis_name='dp')]
  transfers between devices with their start and end apart: 2 -> 3, of which waited for: 1 -> 3; matrix products, arithmetic and copies ran while one was open for 12% -> 11% of each run, Pallas kernels for 0% -> 0%
where the time goes in v1:
time: 200 us; the launch traced here: 199 us
  waiting for transfers between devices  55.3 us (28%)
  matrix products  40.9 us (20%)
  other arithmetic  35.2 us (18%)
  blocking collectives  26.4 us (13%)
  local copies, waits for them, and re-layouts  24.1 us (12%)
  between operations  13.9 us (7%)
  loops' own time  2.88 us (1%)
    psum x1, waiting for transfers between devices, on_device(): lax.psum(weight_part, axis_name='dp')  33.7 us
    scatter-add x1, other arithmetic, on_device(): holder = holder.at[target, :, head_rows, :].add(paired_all, mode='drop')  19 us
    dot_general x4, matrix products, tile_math(): jnp.einsum('ikgd,knjd->kginj', grad_output, value_tile, preferred_element...  16.1 us
    reduce_scatter x1, waiting for transfers between devices, on_device(): lax.psum_scatter(holder.reshape(tokens_here * lax.axis_size('seq'), kv_he...  15.2 us
    all_gather x1, blocking collectives, on_device(): every_logit = lax.all_gather(logit_rows, 'head', axis=1, tiled=True)  13.6 us
    dynamic_slice x16, local copies, waits for them, and re-layouts, on_device(): lax.scan(tile_step, jnp.zeros((), jnp.float32), tile_items)  10.6 us
    dot_general x4, matrix products, tile_math(): jnp.einsum('kginj,ikgd->knjd', prob_low, grad_output, preferred_element_t...  9.55 us
    all_gather x1, blocking collectives, on_device(): lax.all_gather(keys, 'seq', axis=1, tiled=True)  7.12 us
  transfers between devices with their start and end apart: 3, of which 3 were waited for; matrix products, arithmetic and copies ran while one was open for 11% of the time, Pallas kernels for 0%

profile of v1, /device:TPU:0, one launch (start us, length us, event | category | flops | bytes accessed | tf_op | source)
XLA Modules:
  0.0 198.7 jit_solution(16943469141684067259)
XLA Ops:
  8.2 7.1 %all_gather.9 = bf16[1,512,2,128]{3,1,2,0:T(8,128)(2,1)S(1)} all-gather(bf16[1,256,2,128]{3,1,2,0:T(8,128)(2,1)S(1)} %copy.32), channel_id=1, replica_groups=mesh['seq'=2,'head'=4,'dp'=4] {'seq'}, dimensions={1}, use_global_device_ids=true | all-gather | bytes 393216 | tf_op jit(solution)/shard_map/all_gather | solution.py:35
  18.6 5.6 %all_gather.10 = bf16[1,512,2,128]{3,1,2,0:T(8,128)(2,1)S(1)} all-gather(bf16[1,256,2,128]{3,1,2,0:T(8,128)(2,1)S(1)} %copy.35), channel_id=1, replica_groups=mesh['seq'=2,'head'=4,'dp'=4] {'seq'}, dimensions={1}, use_global_device_ids=true | all-gather | bytes 393216 | tf_op jit(solution)/shard_map/all_gather | solution.py:36
  25.3 2.3 %gather_fusion.1 = bf16[128,64,128]{2,1,0:T(8,128)(2,1)} fusion(bf16[8,64,2,128]{3,1,2,0:T(8,128)(2,1)S(1)} %copy.36, s32[128]{0:T(128)S(1)} %reshape.124), kind=kCustom, calls=%fused_computation.1 | custom fusion | bytes 4195328 | tf_op jit(solution)/shard_map/gather | solution.py:41
  27.7 69.9 %while.16 = (s32[]{:T(128)}, bf16[4,64,2,8,128]{4,3,2,1,0:T(8,128)(2,1)}, bf16[4,64,2,8]{1,3,2,0:T(8,128)(2,1)S(1)}, f32[4,2,16,64,256]{4,3,2,1,0:T(8,128)}, bf1...) while((s32[]{:T(128)}, ...), condition=%wide.region_3.4_spmd.clone.clone, body=%wide.region_0.3_spmd.clone.clone.sunk | while | flops 1355944064 | bytes 33248452 | solution.py:120
  34.1 4.0 %fusion.82 = bf16[2,8,64,16,64]{2,4,1,3,0:T(8,128)(2,1)S(1)} fusion(f32[2,16,64,64,8]{3,2,4,1,0:T(8,128)S(1)} %fusion.78, f32[2,8,64]{2,1,0:T(8,128)S(1)} %bitcast.222, f32[2,8,64]{2,1,0:T(8,128)S(1)} %bitcast.223, pred[2,64,16,64]{1,3,2,0:T(8,128)(4,1)S(1)} %compare_and_fusion.2, bf16[4,2,16,64,128]{4,3,2,1,0:T(8,128)(2,1)} %get-tuple-element.380, ...), kind=kOutput, calls=%fused_computation.6.clone.1 | convolution fusion | flops 275120128 | bytes 7221252 | tf_op jit(solution)/shard_map/while/body/eval_jaxpr/ikgd,knjd->kginj/dot_general | solution.py:86
  40.4 2.4 %fusion.85 = f32[2,16,64,128]{3,2,1,0:T(8,128)S(1)} fusion(f32[2,16,64,64,8]{3,2,4,1,0:T(8,128)S(1)} %fusion.78, f32[2,8,64]{2,1,0:T(8,128)S(1)} %bitcast.224, pred[2,64,16,64]{1,3,2,0:T(8,128)(4,1)S(1)} %compare_and_fusion.2, f32[64,2,8]{0,2,1:T(8,128)S(1)} %bitcast.216, bf16[1,64,2,8,128]{4,3,2,1,0:T(8,128)(2,1)S(1)} %get-tuple-element.332), kind=kOutput, calls=%fused_computation.17.clone.1 | convolution fusion | flops 273022976 | bytes 5644288 | tf_op jit(solution)/shard_map/while/body/eval_jaxpr/kginj,ikgd->knjd/dot_general | solution.py:99
  43.7 1.5 fusion.87
  51.6 4.0 %fusion.82 = bf16[2,8,64,16,64]{2,4,1,3,0:T(8,128)(2,1)S(1)} fusion(f32[2,16,64,64,8]{3,2,4,1,0:T(8,128)S(1)} %fusion.78, f32[2,8,64]{2,1,0:T(8,128)S(1)} %bitcast.222, f32[2,8,64]{2,1,0:T(8,128)S(1)} %bitcast.223, pred[2,64,16,64]{1,3,2,0:T(8,128)(4,1)S(1)} %compare_and_fusion.2, bf16[4,2,16,64,128]{4,3,2,1,0:T(8,128)(2,1)} %get-tuple-element.380, ...), kind=kOutput, calls=%fused_computation.6.clone.1 | convolution fusion | flops 275120128 | bytes 7221252 | tf_op jit(solution)/shard_map/while/body/eval_jaxpr/ikgd,knjd->kginj/dot_general | solution.py:86
  55.6 1.3 fusion.83
  57.9 2.4 %fusion.85 = f32[2,16,64,128]{3,2,1,0:T(8,128)S(1)} fusion(f32[2,16,64,64,8]{3,2,4,1,0:T(8,128)S(1)} %fusion.78, f32[2,8,64]{2,1,0:T(8,128)S(1)} %bitcast.224, pred[2,64,16,64]{1,3,2,0:T(8,128)(4,1)S(1)} %compare_and_fusion.2, f32[64,2,8]{0,2,1:T(8,128)S(1)} %bitcast.216, bf16[1,64,2,8,128]{4,3,2,1,0:T(8,128)(2,1)S(1)} %get-tuple-element.332), kind=kOutput, calls=%fused_computation.17.clone.1 | convolution fusion | flops 273022976 | bytes 5644288 | tf_op jit(solution)/shard_map/while/body/eval_jaxpr/kginj,ikgd->knjd/dot_general | solution.py:99
  61.2 1.4 fusion.87
  69.0 4.0 %fusion.82 = bf16[2,8,64,16,64]{2,4,1,3,0:T(8,128)(2,1)S(1)} fusion(f32[2,16,64,64,8]{3,2,4,1,0:T(8,128)S(1)} %fusion.78, f32[2,8,64]{2,1,0:T(8,128)S(1)} %bitcast.222, f32[2,8,64]{2,1,0:T(8,128)S(1)} %bitcast.223, pred[2,64,16,64]{1,3,2,0:T(8,128)(4,1)S(1)} %compare_and_fusion.2, bf16[4,2,16,64,128]{4,3,2,1,0:T(8,128)(2,1)} %get-tuple-element.380, ...), kind=kOutput, calls=%fused_computation.6.clone.1 | convolution fusion | flops 275120128 | bytes 7221252 | tf_op jit(solution)/shard_map/while/body/eval_jaxpr/ikgd,knjd->kginj/dot_general | solution.py:86
  75.3 2.4 %fusion.85 = f32[2,16,64,128]{3,2,1,0:T(8,128)S(1)} fusion(f32[2,16,64,64,8]{3,2,4,1,0:T(8,128)S(1)} %fusion.78, f32[2,8,64]{2,1,0:T(8,128)S(1)} %bitcast.224, pred[2,64,16,64]{1,3,2,0:T(8,128)(4,1)S(1)} %compare_and_fusion.2, f32[64,2,8]{0,2,1:T(8,128)S(1)} %bitcast.216, bf16[1,64,2,8,128]{4,3,2,1,0:T(8,128)(2,1)S(1)} %get-tuple-element.332), kind=kOutput, calls=%fused_computation.17.clone.1 | convolution fusion | flops 273022976 | bytes 5644288 | tf_op jit(solution)/shard_map/while/body/eval_jaxpr/kginj,ikgd->knjd/dot_general | solution.py:99
  78.7 1.5 fusion.87
  86.5 4.0 %fusion.82 = bf16[2,8,64,16,64]{2,4,1,3,0:T(8,128)(2,1)S(1)} fusion(f32[2,16,64,64,8]{3,2,4,1,0:T(8,128)S(1)} %fusion.78, f32[2,8,64]{2,1,0:T(8,128)S(1)} %bitcast.222, f32[2,8,64]{2,1,0:T(8,128)S(1)} %bitcast.223, pred[2,64,16,64]{1,3,2,0:T(8,128)(4,1)S(1)} %compare_and_fusion.2, bf16[4,2,16,64,128]{4,3,2,1,0:T(8,128)(2,1)} %get-tuple-element.380, ...), kind=kOutput, calls=%fused_computation.6.clone.1 | convolution fusion | flops 275120128 | bytes 7221252 | tf_op jit(solution)/shard_map/while/body/eval_jaxpr/ikgd,knjd->kginj/dot_general | solution.py:86
  90.5 1.3 fusion.83
  92.8 2.4 %fusion.85 = f32[2,16,64,128]{3,2,1,0:T(8,128)S(1)} fusion(f32[2,16,64,64,8]{3,2,4,1,0:T(8,128)S(1)} %fusion.78, f32[2,8,64]{2,1,0:T(8,128)S(1)} %bitcast.224, pred[2,64,16,64]{1,3,2,0:T(8,128)(4,1)S(1)} %compare_and_fusion.2, f32[64,2,8]{0,2,1:T(8,128)S(1)} %bitcast.216, bf16[1,64,2,8,128]{4,3,2,1,0:T(8,128)(2,1)S(1)} %get-tuple-element.332), kind=kOutput, calls=%fused_computation.17.clone.1 | convolution fusion | flops 273022976 | bytes 5644288 | tf_op jit(solution)/shard_map/while/body/eval_jaxpr/kginj,ikgd->knjd/dot_general | solution.py:99
  96.1 1.5 fusion.87
  97.7 13.6 %all-gather = bf16[64,256]{1,0:T(8,128)(2,1)S(1)} all-gather(bf16[16,256]{1,0:T(8,128)(2,1)S(1)} %bitcast.227), channel_id=2, replica_groups=mesh['seq'=2,'head'=4,'dp'=4] {'head'}, dimensions={0}, use_global_device_ids=true | all-gather | bytes 40960 | tf_op jit(solution)/shard_map/all_gather | solution.py:138
  112.4 33.7 %all-reduce.3.cloned.1.call-done = f32[64,1280]{1,0:T(8,128)} async-done(((f32[64,1280]{1,0:T(8,128)}), f32[64,1280]{1,0:T(8,128)}) %all-reduce.3.cloned.1.call-update) | async-done | bytes 327696 | tf_op jit(solution)/shard_map/psum | solution.py:142
  146.3 19.0 %scatter_fusion = f32[8,64,2,256]{3,1,2,0:T(8,128)S(1)} fusion(f32[8,64,2,256]{3,1,2,0:T(8,128)S(1)} %broadcast_in_dim.53, s32[128]{0:T(128)S(1)} %reshape.136, f32[128,64,256]{2,1,0:T(8,128)} %bitcast.210), kind=kCustom, calls=%fused_computation.2 | custom fusion | flops 2097152 | bytes 25166848 | tf_op jit(solution)/shard_map/scatter-add | solution.py:127
  166.3 6.4 %all-reduce.5.cloned.1.call-done = f32[64,1280]{1,0:T(8,128)} async-done(((f32[64,1280]{1,0:T(8,128)}), f32[64,1280]{1,0:T(8,128)}) %all-reduce.5.cloned.1.call-update) | async-done | bytes 327696 | tf_op jit(solution)/shard_map/psum | solution.py:142
  172.7 1.7 broadcast_multiply_fusion
  174.4 15.2 %reduce-scatter.2.cloned.1.call-done = bf16[256,2,256]{2,0,1:T(8,128)(2,1)} async-done(((bf16[512,2,256]{2,0,1:T(8,128)(2,1)}), bf16[256,2,256]{2,0,1:T(8,128)(2,1)}) %reduce-scatter.2.cloned.1.call-update) | async-done | bytes 262160 | tf_op jit(solution)/shard_map/reduce_scatter | solution.py:128
  (92 shorter events, 43.0 us)
Async XLA Ops:
  7.2 104.2 %copy-start = (bf16[1,256,1280]{2,1,0:T(8,128)(2,1)S(1)}, bf16[1,256,1280]{2,1,0:T(8,128)(2,1)}, u32[]{:S(2)}) copy-start(bf16[1,256,1280]{2,1,0:T(8,128)(2,1)} %param.19) | copy-start | bytes 1966084
  7.2 20.5 %copy-start.1 = (f32[1,16,256]{2,1,0:T(8,128)S(1)}, f32[1,16,256]{2,1,0:T(8,128)}, u32[]{:S(2)}) copy-start(f32[1,16,256]{2,1,0:T(8,128)} %param.17) | copy-start | bytes 49156
  7.2 138.9 %all-reduce.3.cloned.1.call-start = ((), (), s32[]{:S(2)}) async-start(), calls=%async_computation.2 | async-start | bytes 655360 | tf_op jit(solution)/shard_map/psum | solution.py:142
  112.3 60.4 %all-reduce.5.cloned.1.call-start = ((), (), s32[]{:S(2)}) async-start(), calls=%async_computation.3 | async-start | bytes 655360 | tf_op jit(solution)/shard_map/psum | solution.py:142
  146.1 43.6 %reduce-scatter.2.cloned.1.call-start = ((), (), s32[]{:S(2)}) async-start(), calls=%async_computation.1 | async-start | bytes 786432 | tf_op jit(solution)/shard_map/reduce_scatter | solution.py:128
Sparse Core Ops, SparseCore 0:
  112.4 33.5 all-reduce.2
  148.3 24.3 all-reduce.4
  175.0 14.6 reduce-scatter.1
